TPU v7x, 256 devices: a whole 4x4x8 slice. The times are simulated.
256 devices in a mesh: trial: 2 (over core), bank: 4 (over x), zero: 32 (over z, y).
Axes of the slice: x: 4, y: 4, z: 8, core: 2. Of those that a mesh axis runs over, the one named last changes fastest.
Arguments:
- w_gate: float32 [128, 2048, 1024], P(('trial', 'bank'), 'zero'), parts along dimension 0, may hold values from -0.25 to 0.25
- w_up: float32 [128, 2048, 1024], P(('trial', 'bank'), 'zero'), parts along dimension 0, may hold values from -0.25 to 0.25
- router_weight: float32 [4096, 64], P(('trial', 'zero'), 'bank'), parts along dimension 0, may hold values from -0.125 to 0.125
- router_gain: float32 [4096], P(('trial', 'zero')), parts along dimension 0, may hold values from 0.25 to 1.75
Outputs:
- serve_gate: bfloat16 [128, 2048, 1024], P(('trial', 'bank'), None, 'zero'), parts along dimension 0
- serve_up: bfloat16 [128, 2048, 1024], P(('trial', 'bank'), None, 'zero'), parts along dimension 0
- scale_gate: float32 [128, 1024], P(('trial', 'bank'), 'zero'), parts along dimension 0
- scale_up: float32 [128, 1024], P(('trial', 'bank'), 'zero'), parts along dimension 0
- serve_router: bfloat16 [4096, 64], P('trial'), parts along dimension 0
There are 2 independent parts, one for each index of `trial`. A program takes and returns all parts, laid end to end along the dimension named above; each array names one. Nothing has to cross between parts.
All inputs are finite; a program needn't handle non-finite values. Where the computation divides by a largest or mean magnitude, that divisor is 1e-20 or more.
Results may differ from a plain program's by a relative error of at most 0.001.
Values may be sent and summed in bfloat16 or wider, within the bound.
A program may use at most 128 MiB of HBM per device.

v0:
```python
import jax
import jax.numpy as jnp
from jax import lax
from jax.sharding import PartitionSpec as P

D_MODEL = 2048


def rows_for(lines, count):
    spare = -lines.shape[0] % count
    if not spare:
        return lines
    return jnp.concatenate([lines, jnp.zeros((spare, *lines.shape[1:]), lines.dtype)])


def sent_to_all(array, axis):
    count = lax.axis_size(axis)
    return lax.all_to_all(
        jnp.broadcast_to(array[None], (count, *array.shape)), axis, 0, 0, tiled=True
    )


def laid_out(tiles, dim):
    dims = list(tiles.shape[1:])
    dims[dim] *= tiles.shape[0]
    return jnp.moveaxis(tiles, 0, dim).reshape(dims)


def gathered_copies(array, axis, dim):
    tiles = sent_to_all(array, axis)
    return laid_out(tiles, dim)


def in_blocks(array, dim, count):
    dims = array.shape
    tiles = array.reshape(*dims[:dim], count, dims[dim] // count, *dims[dim + 1 :])
    return jnp.moveaxis(tiles, dim, 0)


def summed_on_arrival(array, axis, dim):
    tiles = in_blocks(array, dim, lax.axis_size(axis))
    arrived = lax.all_to_all(tiles, axis, split_axis=0, concat_axis=0, tiled=True)
    return arrived.sum(axis=0)


def total_of(array, axes):
    padded = rows_for(array, lax.axis_size(axes))
    whole = gathered_copies(summed_on_arrival(padded, axes, 0), axes, 0)
    return lax.slice_in_dim(whole, 0, len(array)).reshape(array.shape)


def packed_total(arrays, axis):
    ravelled, at, finished = (jnp.concatenate([a.reshape(-1) for a in arrays]), 0, [])
    total = total_of(ravelled, axis)
    for a in arrays:
        finished.append(total[at : at + a.size].reshape(a.shape))
        at += a.size
    return tuple(finished)


def local(w_gate, w_up, router_weight, router_gain):
    total_gate, total_up = packed_total(
        (jnp.sum(jnp.abs(w_gate), axis=1), jnp.sum(jnp.abs(w_up), axis=1)), "zero"
    )
    scale_gate = total_gate / D_MODEL
    scale_up = total_up / D_MODEL
    narrow_gate, narrow_up = (
        (w_gate / jnp.expand_dims(scale_gate, 1)).astype(jnp.bfloat16),
        (w_up / jnp.expand_dims(scale_up, 1)).astype(jnp.bfloat16),
    )
    serve_gate, serve_up = (
        lax.all_to_all(narrow_gate, "zero", split_axis=2, concat_axis=1, tiled=True),
        lax.all_to_all(narrow_up, "zero", split_axis=2, concat_axis=1, tiled=True),
    )
    scale_gate = lax.dynamic_slice_in_dim(
        scale_gate, lax.axis_index("zero") * serve_gate.shape[2], serve_gate.shape[2], axis=1
    )
    scale_up = lax.dynamic_slice_in_dim(
        scale_up, lax.axis_index("zero") * serve_up.shape[2], serve_up.shape[2], axis=1
    )
    part_router = (router_weight * router_gain[:, None]).astype(jnp.bfloat16)
    row_router = gathered_copies(part_router, "zero", 0)
    serve_router = gathered_copies(row_router, "bank", 1)
    return (serve_gate, serve_up, scale_gate, scale_up, serve_router)


def solution(mesh):
    placed = (
        P(("trial", "bank"), "zero", None),
        P(("trial", "bank"), "zero", None),
        P(("trial", "zero"), "bank"),
        P(("trial", "zero")),
    )
    return jax.shard_map(
        local,
        mesh=mesh,
        in_specs=placed,
        out_specs=(
            P(("trial", "bank"), None, "zero"),
            P(("trial", "bank"), None, "zero"),
            P(("trial", "bank"), "zero"),
            P(("trial", "bank"), "zero"),
            P("trial", None),
        ),
        check_vma=False,
    )
```

profile of v0, /device:TPU:10, one launch (start us, length us, event | category | flops | bytes accessed | tf_op | source)
XLA Modules:
  0.0 207.8 jit_solution(914936306891506960)
XLA Ops:
  0.6 0.0 copy-start
  0.6 0.0 copy-start.1
  0.7 5.0 %abs_reduce_fusion = (f32[16,1024]{1,0:T(8,128)S(1)}, f32[16,1024]{1,0:T(8,128)S(1)}) fusion(f32[16,64,1024]{2,1,0:T(8,128)} %param.5, f32[16,64,1024]{2,1,0:T(8,128)} %param.4), kind=kLoop, calls=%fused_computation.2 | loop fusion | flops 4161536 | bytes 8519680 | tf_op jit(solution)/shard_map/reduce_sum | solution.py:63
  5.7 0.7 all_to_all.42
  6.5 11.7 %all-to-all-start = ((f32[32,1,1024]{2,1,0:T(1,128)}), f32[32,1,1024]{2,1,0:T(1,128)S(1)}, u32[]{:S(2)}, u32[]{:S(2)}) async-start(f32[32,1,1024]{2,1,0:T(1,128)} %all_to_all.42), calls=%async_computation | async-start | bytes 262144 | tf_op jit(solution)/shard_map/all_to_all | solution.py:42
  18.2 0.0 copy-done
  18.2 0.0 copy-done.1
  18.2 0.8 reshape.53
  19.0 8.0 %all-to-all-done = f32[32,1,1024]{2,1,0:T(1,128)S(1)} async-done(((f32[32,1,1024]{2,1,0:T(1,128)}), f32[32,1,1024]{2,1,0:T(1,128)S(1)}, u32[]{:S(2)}, u32[]{:S(2)}) %all-to-all-start) | async-done | bytes 131104 | tf_op jit(solution)/shard_map/all_to_all | solution.py:42
  27.0 5.3 %all-to-all-start.4 = ((bf16[32,2,512]{2,1,0:T(2,128)(2,1)}), bf16[32,2,512]{2,1,0:T(2,128)(2,1)S(1)}, u32[]{:S(2)}, u32[]{:S(2)}) async-start(bf16[32,2,512]{2,1,0:T(2,128)(2,1)} %reshape.53), calls=%async_computation.4 | async-start | bytes 131072 | tf_op jit(solution)/shard_map/all_to_all | solution.py:18
  32.4 0.1 reduce_sum.29
  32.5 8.6 %all-to-all-done.4 = bf16[32,2,512]{2,1,0:T(2,128)(2,1)S(1)} async-done(((bf16[32,2,512]{2,1,0:T(2,128)(2,1)}), bf16[32,2,512]{2,1,0:T(2,128)(2,1)S(1)}, u32[]{:S(2)}, u32[]{:S(2)}) %all-to-all-start.4) | async-done | bytes 65568 | tf_op jit(solution)/shard_map/all_to_all | solution.py:18
  41.1 0.7 broadcast_in_dim.8
  41.8 5.2 %all-to-all-start.1 = ((f32[32,1,1024]{2,1,0:T(1,128)}), f32[32,1,1024]{2,1,0:T(1,128)S(1)}, u32[]{:S(2)}, u32[]{:S(2)}) async-start(f32[32,1,1024]{2,1,0:T(1,128)} %broadcast_in_dim.8), calls=%async_computation.1 | async-start | bytes 262144 | tf_op jit(solution)/shard_map/all_to_all | solution.py:18
  47.0 8.1 %copy.30 = f32[16,64,1024]{1,0,2:T(8,128)} copy(f32[16,64,1024]{2,1,0:T(8,128)} %param.5) | data formatting | bytes 8388608 | tf_op args[1]
  55.1 0.1 reshape.54
  55.3 0.2 broadcast_in_dim.10
  55.5 0.5 all-to-all-done.1
  56.0 0.7 broadcast_in_dim.11
  56.7 4.8 %all-to-all-start.5 = ((bf16[4,2048,16]{1,2,0:T(8,128)(2,1)}), bf16[4,2048,16]{1,2,0:T(8,128)(2,1)S(1)}, u32[]{:S(2)}, u32[]{:S(2)}) async-start(bf16[4,2048,16]{1,2,0:T(8,128)(2,1)} %broadcast_in_dim.11), calls=%async_computation.5 | async-start | bytes 524288 | tf_op jit(solution)/shard_map/all_to_all | solution.py:18
  61.5 0.1 slice_multiply_fusion
  61.7 0.2 copy.36
  61.9 6.9 %fusion.1 = bf16[1024,16,64]{2,1,0:T(8,128)(2,1)} fusion(f32[16,64,1024]{1,0,2:T(8,128)} %copy.30, f32[16,1024]{0,1:T(8,128)S(1)} %bitcast.34), kind=kLoop, calls=%fused_computation.11 | loop fusion | flops 2097152 | bytes 6356992
  68.8 7.9 %reshape.51 = bf16[32,2,16384]{2,1,0:T(2,128)(2,1)} reshape(bf16[1024,16,64]{2,1,0:T(8,128)(2,1)} %fusion.1) | data formatting | bytes 4194304
  76.6 0.0 all-to-all-done.5
  76.6 9.4 %all-to-all-start.3 = ((bf16[32,2,16384]{2,1,0:T(2,128)(2,1)}), bf16[32,2,16384]{2,1,0:T(2,128)(2,1)S(1)}, u32[]{:S(2)}, u32[]{:S(2)}) async-start(bf16[32,2,16384]{2,1,0:T(2,128)(2,1)} %reshape.51), calls=%async_computation.3 | async-start | bytes 4194304 | tf_op jit(solution)/shard_map/all_to_all | solution.py:73
  86.0 8.1 %copy.26 = f32[16,64,1024]{1,0,2:T(8,128)} copy(f32[16,64,1024]{2,1,0:T(8,128)} %param.4) | data formatting | bytes 8388608 | tf_op args[0]
  94.1 0.2 copy.34
  94.3 6.9 %fusion = bf16[1024,16,64]{2,1,0:T(8,128)(2,1)} fusion(f32[16,64,1024]{1,0,2:T(8,128)} %copy.26, f32[16,1024]{0,1:T(8,128)S(1)} %bitcast.35), kind=kLoop, calls=%fused_computation.10 | loop fusion | flops 2097152 | bytes 6356992
  101.2 7.9 %reshape.49 = bf16[32,2,16384]{2,1,0:T(2,128)(2,1)} reshape(bf16[1024,16,64]{2,1,0:T(8,128)(2,1)} %fusion) | data formatting | bytes 4194304
  109.1 24.1 %all-to-all-done.3 = bf16[32,2,16384]{2,1,0:T(2,128)(2,1)S(1)} async-done(((bf16[32,2,16384]{2,1,0:T(2,128)(2,1)}), bf16[32,2,16384]{2,1,0:T(2,128)(2,1)S(1)}, u32[]{:S(2)}, u32[]{:S(2)}) %all-to-all-start.3) | async-done | bytes 2097184 | tf_op jit(solution)/shard_map/all_to_all | solution.py:73
  133.2 5.6 %all-to-all-start.2 = ((bf16[32,2,16384]{2,1,0:T(2,128)(2,1)}), bf16[32,2,16384]{2,1,0:T(2,128)(2,1)}, u32[]{:S(2)}, u32[]{:S(2)}) async-start(bf16[32,2,16384]{2,1,0:T(2,128)(2,1)} %reshape.49), calls=%async_computation.2 | async-start | bytes 4194304 | tf_op jit(solution)/shard_map/all_to_all | solution.py:72
  138.8 0.7 constant_dynamic-slice_fusion.1
  139.5 0.7 constant_dynamic-slice_fusion
  140.2 4.0 %reshape.52 = bf16[1024,16,64]{2,1,0:T(8,128)(2,1)} reshape(bf16[32,2,16384]{2,1,0:T(2,128)(2,1)S(1)} %all-to-all-done.3) | data formatting | bytes 4194304
  144.2 6.9 %copy.32 = bf16[16,32,64,32]{2,1,3,0:T(8,128)(2,1)} copy(bf16[16,32,64,32]{2,0,3,1:T(8,128)(2,1)} %bitcast.32) | data formatting | bytes 4194304 | tf_op jit(solution)/shard_map/all_to_all | solution.py:73
  151.1 6.7 %all_to_all.52 = bf16[16,2048,32]{1,2,0:T(8,128)(2,1)} reshape(bf16[16,32,64,32]{2,1,3,0:T(8,128)(2,1)} %copy.32) | data formatting | bytes 4194304 | tf_op jit(solution)/shard_map/all_to_all | solution.py:73
  157.8 27.8 %all-to-all-done.2 = bf16[32,2,16384]{2,1,0:T(2,128)(2,1)} async-done(((bf16[32,2,16384]{2,1,0:T(2,128)(2,1)}), bf16[32,2,16384]{2,1,0:T(2,128)(2,1)}, u32[]{:S(2)}, u32[]{:S(2)}) %all-to-all-start.2) | async-done | bytes 2097184 | tf_op jit(solution)/shard_map/all_to_all | solution.py:72
  185.6 7.9 %reshape.50 = bf16[1024,16,64]{2,1,0:T(8,128)(2,1)} reshape(bf16[32,2,16384]{2,1,0:T(2,128)(2,1)} %all-to-all-done.2) | data formatting | bytes 4194304
  193.5 6.9 %copy.28 = bf16[16,32,64,32]{2,1,3,0:T(8,128)(2,1)} copy(bf16[16,32,64,32]{2,0,3,1:T(8,128)(2,1)} %bitcast.33) | data formatting | bytes 4194304 | tf_op jit(solution)/shard_map/all_to_all | solution.py:72
  200.4 6.7 %all_to_all.48 = bf16[16,2048,32]{1,2,0:T(8,128)(2,1)} reshape(bf16[16,32,64,32]{2,1,3,0:T(8,128)(2,1)} %copy.28) | data formatting | bytes 4194304 | tf_op jit(solution)/shard_map/all_to_all | solution.py:72
  207.1 0.7 copy.39
  (4 shorter events, 0.1 us)
Async XLA Ops:
  0.6 17.5 %copy-start = (f32[64,16]{0,1:T(8,128)S(1)}, f32[64,16]{0,1:T(8,128)}, u32[]{:S(2)}) copy-start(f32[64,16]{0,1:T(8,128)} %param.6) | copy-start | bytes 12292
  0.6 17.5 %copy-start.1 = (f32[64]{0:T(128)S(1)}, f32[64]{0:T(128)}, u32[]{:S(2)}) copy-start(f32[64]{0:T(128)} %param.7) | copy-start | bytes 772
  6.5 20.6 %all-to-all-start = ((f32[32,1,1024]{2,1,0:T(1,128)}), f32[32,1,1024]{2,1,0:T(1,128)S(1)}, u32[]{:S(2)}, u32[]{:S(2)}) async-start(f32[32,1,1024]{2,1,0:T(1,128)} %all_to_all.42), calls=%async_computation | async-start | bytes 262144 | tf_op jit(solution)/shard_map/all_to_all | solution.py:42
  27.0 14.1 %all-to-all-start.4 = ((bf16[32,2,512]{2,1,0:T(2,128)(2,1)}), bf16[32,2,512]{2,1,0:T(2,128)(2,1)S(1)}, u32[]{:S(2)}, u32[]{:S(2)}) async-start(bf16[32,2,512]{2,1,0:T(2,128)(2,1)} %reshape.53), calls=%async_computation.4 | async-start | bytes 131072 | tf_op jit(solution)/shard_map/all_to_all | solution.py:18
  41.8 14.2 %all-to-all-start.1 = ((f32[32,1,1024]{2,1,0:T(1,128)}), f32[32,1,1024]{2,1,0:T(1,128)S(1)}, u32[]{:S(2)}, u32[]{:S(2)}) async-start(f32[32,1,1024]{2,1,0:T(1,128)} %broadcast_in_dim.8), calls=%async_computation.1 | async-start | bytes 262144 | tf_op jit(solution)/shard_map/all_to_all | solution.py:18
  56.7 19.9 %all-to-all-start.5 = ((bf16[4,2048,16]{1,2,0:T(8,128)(2,1)}), bf16[4,2048,16]{1,2,0:T(8,128)(2,1)S(1)}, u32[]{:S(2)}, u32[]{:S(2)}) async-start(bf16[4,2048,16]{1,2,0:T(8,128)(2,1)} %broadcast_in_dim.11), calls=%async_computation.5 | async-start | bytes 524288 | tf_op jit(solution)/shard_map/all_to_all | solution.py:18
  76.6 56.5 %all-to-all-start.3 = ((bf16[32,2,16384]{2,1,0:T(2,128)(2,1)}), bf16[32,2,16384]{2,1,0:T(2,128)(2,1)S(1)}, u32[]{:S(2)}, u32[]{:S(2)}) async-start(bf16[32,2,16384]{2,1,0:T(2,128)(2,1)} %reshape.51), calls=%async_computation.3 | async-start | bytes 4194304 | tf_op jit(solution)/shard_map/all_to_all | solution.py:73
  133.2 52.4 %all-to-all-start.2 = ((bf16[32,2,16384]{2,1,0:T(2,128)(2,1)}), bf16[32,2,16384]{2,1,0:T(2,128)(2,1)}, u32[]{:S(2)}, u32[]{:S(2)}) async-start(bf16[32,2,16384]{2,1,0:T(2,128)(2,1)} %reshape.49), calls=%async_computation.2 | async-start | bytes 4194304 | tf_op jit(solution)/shard_map/all_to_all | solution.py:72
where the time goes:
time: 209 us; the launch traced here: 208 us
  local copies, waits for them, and re-layouts  76.9 us (37%)
  waiting for transfers between devices  69.1 us (33%)
  starting transfers between devices  42 us (20%)
  other arithmetic  19 us (9%)
    unnamed x14, local copies, waits for them, and re-layouts  45.5 us
    all_to_all x1, waiting for transfers between devices, local(): lax.all_to_all(narrow_gate, 'zero', split_axis=2, concat_axis=1, tiled=True)  27.8 us
    all_to_all x1, waiting for transfers between devices, local(): lax.all_to_all(narrow_up, 'zero', split_axis=2, concat_axis=1, tiled=True)  24.1 us
    all_to_all x3, starting transfers between devices, sent_to_all(): lax.all_to_all(jnp.broadcast_to(array[None], (count, *array.shape)), axis...  15.3 us
    unnamed x2, other arithmetic  13.8 us
    all_to_all x2, local copies, waits for them, and re-layouts, local(): lax.all_to_all(narrow_up, 'zero', split_axis=2, concat_axis=1, tiled=True)  13.6 us
    all_to_all x2, local copies, waits for them, and re-layouts, local(): lax.all_to_all(narrow_gate, 'zero', split_axis=2, concat_axis=1, tiled=True)  13.6 us
    all_to_all x1, starting transfers between devices, summed_on_arrival(): lax.all_to_all(tiles, axis, split_axis=0, concat_axis=0, tiled=True)  11.7 us
  transfers between devices with their start and end apart: 6, of which 5 were waited for; matrix products, arithmetic and copies ran while one was open for 29% of the time, Pallas kernels for 0%

commit v1 on v0

v1 whole, which is shorter than its diff:
```python
import functools

import jax
import jax.numpy as jnp
from jax import lax
from jax.experimental import pallas as pl
from jax.experimental.pallas import tpu as pltpu
from jax.sharding import PartitionSpec as P

MESH = pl.DeviceIdType.MESH
D_MODEL = 2048
PEERS = 32
BANKS = 4
MATS = 32
PAIRS = MATS // 2
COLS = 32
CHUNKS = ((0, 1), (1, 1), (2, 2), (4, 4), (8, 4), (12, 4))
LOADS = 8


def far_first(k, me):
    t, u = k // 4, lax.rem(k, 4)
    dz = 4 + (2 * lax.rem(t, 2) - 1) * ((t + 1) // 2)
    dy = 2 + (2 * lax.rem(u, 2) - 1) * ((u + 1) // 2)
    z, y = me // 4, lax.rem(me, 4)
    return lax.rem(z + dz, 8) * 4 + lax.rem(y + dy, 4)


def spread_kernel(
    gate, up, router, gain,
    rx, scales, router_out,
    w, rs_tx, rs_rx, ag_tx, ag_rx, tx, rt_tx, rt_rx,
    load_sem, rs_send, rs_recv, ag_send, ag_recv, rt_send, rt_recv, x_send, x_recv, send, recv,
):
    me, bank = lax.axis_index("zero"), lax.axis_index("bank")

    per = MATS // LOADS
    loads = []
    for n in range(LOADS):
        source = gate if n < LOADS // 2 else up
        first = n % (LOADS // 2) * per
        copy = pltpu.make_async_copy(
            source.at[pl.ds(first, per)], w.at[pl.ds(n * per, per)], load_sem.at[n]
        )
        copy.start()
        loads.append(copy)

    barrier = pltpu.get_barrier_semaphore()

    @pl.loop(0, PEERS - 1)
    def _(k):
        pl.semaphore_signal(
            barrier, inc=1, device_id={"zero": far_first(k, me)}, device_id_type=MESH
        )

    for hop in range(1, BANKS):
        pl.semaphore_signal(
            barrier, inc=1, device_id={"bank": lax.rem(bank + hop, BANKS)}, device_id_type=MESH
        )

    lane = lax.broadcasted_iota(jnp.int32, (8, 128), 1) // 32

    parts = []
    for n in range(LOADS):
        loads[n].wait()
        parts.append(jnp.sum(jnp.abs(w[n * per : (n + 1) * per]), axis=1))
    sums = jnp.concatenate(parts, axis=0)
    for q in range(8):
        blocks = [sums[8 * a : 8 * a + 8, 128 * q : 128 * q + 128] for a in range(4)]
        for r in range(4):
            tile = None
            for a in range(4):
                moved = pltpu.roll(blocks[a], (32 * (a - r)) % 128, 1) if a != r else blocks[a]
                tile = moved if tile is None else jnp.where(lane == a, moved, tile)
            rs_tx[4 * q + r] = tile

    made = router[...] * gain[...]
    rt_tx[...] = jnp.concatenate([made[:8], made[8:]], axis=1).astype(jnp.bfloat16)

    pl.semaphore_wait(barrier, PEERS - 1 + BANKS - 1)

    def to_peer(k, src, dst, send_sem, recv_sem):
        peer = far_first(k, me)
        pltpu.make_async_remote_copy(
            src_ref=src(peer), dst_ref=dst, send_sem=send_sem, recv_sem=recv_sem,
            device_id={"zero": peer}, device_id_type=MESH,
        ).start()

    def bytes_of(ref, sem):
        pltpu.make_async_copy(ref, ref, sem).wait()

    others = pl.ds(0, PEERS - 1)

    @pl.loop(0, PEERS - 1)
    def _(k):
        to_peer(k, lambda peer: rs_tx.at[peer], rs_rx.at[me], rs_send, rs_recv)

    @pl.loop(0, PEERS - 1)
    def _(k):
        to_peer(k, lambda peer: rt_tx, rt_rx.at[me], rt_send, rt_recv)

    rs_rx[me] = rs_tx[me]
    rt_rx[me] = rt_tx[...]

    bytes_of(rs_rx.at[others], rs_recv)
    scale = jnp.sum(rs_rx[...], axis=0) / D_MODEL
    scales[...] = scale
    ag_tx[...] = 1.0 / scale

    @pl.loop(0, PEERS - 1)
    def _(k):
        to_peer(k, lambda peer: ag_tx, ag_rx.at[me], ag_send, ag_recv)

    ag_rx[me] = ag_tx[...]

    bytes_of(rt_rx.at[others], rt_recv)
    for k in range(PEERS // 2):
        a, b = rt_rx[2 * k].astype(jnp.float32), rt_rx[2 * k + 1].astype(jnp.float32)
        low = jnp.concatenate([a[:, :64], b[:, :64]], axis=1)
        high = jnp.concatenate([a[:, 64:], b[:, 64:]], axis=1)
        router_out[bank, :, 128 * k : 128 * k + 128] = jnp.concatenate([low, high], axis=0).astype(
            jnp.bfloat16
        )
    crossing = []
    for hop in range(1, BANKS):
        copy = pltpu.make_async_remote_copy(
            src_ref=router_out.at[bank], dst_ref=router_out.at[bank],
            send_sem=x_send.at[hop - 1], recv_sem=x_recv.at[hop - 1],
            device_id={"bank": lax.rem(bank + hop, BANKS)}, device_id_type=MESH,
        )
        copy.start()
        crossing.append(copy)

    bytes_of(ag_rx.at[others], ag_recv)
    rows = []
    for a in range(4):
        along = []
        for q in range(8):
            block = None
            for r in range(4):
                tile = ag_rx[4 * q + r]
                moved = pltpu.roll(tile, (32 * (r - a)) % 128, 1) if a != r else tile
                block = moved if block is None else jnp.where(lane == r, moved, block)
            along.append(block)
        rows.append(along)

    for c, (first, count) in enumerate(CHUNKS):
        for p in range(first, first + count):
            for q in range(8):
                block = w[2 * p : 2 * p + 2, :, 128 * q : 128 * q + 128]
                g = 2 * p
                factor = rows[g // 8][q][g % 8 : g % 8 + 2]
                turned = (block * factor[:, None, :]).reshape(128, 128).T
                tx[4 * q : 4 * q + 4, p] = turned.astype(jnp.bfloat16).reshape(4, COLS, 128)
        span = pl.ds(first, count)

        @pl.loop(0, PEERS - 1)
        def _(k, span=span, c=c):
            to_peer(
                k, lambda peer: tx.at[peer, span], rx.at[me, span], send.at[c], recv.at[c]
            )

        rx[me, first : first + count] = tx[me, first : first + count]

    for copy in crossing:
        copy.wait()
    for c, (first, count) in enumerate(CHUNKS):
        bytes_of(rx.at[others, pl.ds(first, count)], recv.at[c])
    bytes_of(rs_rx.at[others], rs_send)
    bytes_of(rt_rx.at[others], rt_send)
    bytes_of(ag_rx.at[others], ag_send)
    for c, (first, count) in enumerate(CHUNKS):
        bytes_of(tx.at[others, pl.ds(first, count)], send.at[c])


def place_kernel(rx, scales, router_in, gate, up, scale_gate, scale_up, router, out, sem):
    whole = pltpu.make_async_copy(router_in, router, sem.at[PAIRS])
    whole.start()
    copies = []
    for p in range(PAIRS):
        for k in range(PEERS // 2):
            a, b = rx[2 * k, p].astype(jnp.float32), rx[2 * k + 1, p].astype(jnp.float32)
            here = slice(128 * k, 128 * k + 128)
            even = jnp.concatenate([a[:, :64], b[:, :64]], axis=1)
            odd = jnp.concatenate([a[:, 64:], b[:, 64:]], axis=1)
            out[2 * p, :, here] = even.astype(jnp.bfloat16)
            out[2 * p + 1, :, here] = odd.astype(jnp.bfloat16)
        target, first = (gate, 2 * p) if p < PAIRS // 2 else (up, 2 * p - MATS // 2)
        copy = pltpu.make_async_copy(
            out.at[pl.ds(2 * p, 2)], target.at[pl.ds(first, 2)], sem.at[p]
        )
        copy.start()
        copies.append(copy)
    for a in range(2):
        scale_gate[8 * a : 8 * a + 8] = scales[:, 32 * a : 32 * a + 32]
        scale_up[8 * a : 8 * a + 8] = scales[:, 64 + 32 * a : 96 + 32 * a]
    for copy in copies:
        copy.wait()
    whole.wait()


def local(w_gate, w_up, router_weight, router_gain):
    f32, bf16 = jnp.float32, jnp.bfloat16
    vmem, hbm = pl.BlockSpec(memory_space=pltpu.VMEM), pl.BlockSpec(memory_space=pltpu.HBM)
    dma = pltpu.SemaphoreType.DMA
    rx, scales, router = pl.pallas_call(
        spread_kernel,
        out_shape=(
            jax.ShapeDtypeStruct((PEERS, PAIRS, COLS, 128), bf16),
            jax.ShapeDtypeStruct((8, 128), f32),
            jax.ShapeDtypeStruct((BANKS, 16, D_MODEL), bf16),
        ),
        in_specs=[hbm, hbm, vmem, vmem],
        out_specs=(vmem, vmem, vmem),
        scratch_shapes=[
            pltpu.VMEM((MATS, 64, 1024), f32),
            pltpu.VMEM((PEERS, 8, 128), f32),
            pltpu.VMEM((PEERS, 8, 128), f32),
            pltpu.VMEM((8, 128), f32),
            pltpu.VMEM((PEERS, 8, 128), f32),
            pltpu.VMEM((PEERS, PAIRS, COLS, 128), bf16),
            pltpu.VMEM((8, 128), bf16),
            pltpu.VMEM((PEERS, 8, 128), bf16),
            dma((LOADS,)),
            *[dma(())] * 6,
            dma((BANKS - 1,)),
            dma((BANKS - 1,)),
            dma((len(CHUNKS),)),
            dma((len(CHUNKS),)),
        ],
        compiler_params=pltpu.CompilerParams(
            collective_id=0, has_side_effects=True, vmem_limit_bytes=46 * 2**20
        ),
    )(w_gate, w_up, router_weight.T, router_gain.reshape(1, -1))
    serve_gate, serve_up, scale_gate, scale_up, router = pl.pallas_call(
        place_kernel,
        out_shape=(
            jax.ShapeDtypeStruct((16, COLS, D_MODEL), bf16),
            jax.ShapeDtypeStruct((16, COLS, D_MODEL), bf16),
            jax.ShapeDtypeStruct((16, COLS), f32),
            jax.ShapeDtypeStruct((16, COLS), f32),
            jax.ShapeDtypeStruct((BANKS, 16, D_MODEL), bf16),
        ),
        in_specs=[vmem, vmem, vmem],
        out_specs=(hbm, hbm, vmem, vmem, hbm),
        scratch_shapes=[pltpu.VMEM((MATS, COLS, D_MODEL), bf16), dma((PAIRS + 1,))],
        compiler_params=pltpu.CompilerParams(vmem_limit_bytes=32 * 2**20),
    )(rx, scales, router)
    return (
        jnp.swapaxes(serve_gate, 1, 2),
        jnp.swapaxes(serve_up, 1, 2),
        scale_gate,
        scale_up,
        router.reshape(BANKS * 16, D_MODEL).T,
    )


def solution(mesh):
    placed = (
        P(("trial", "bank"), "zero", None),
        P(("trial", "bank"), "zero", None),
        P(("trial", "zero"), "bank"),
        P(("trial", "zero")),
    )
    return jax.shard_map(
        local,
        mesh=mesh,
        in_specs=placed,
        out_specs=(
            P(("trial", "bank"), None, "zero"),
            P(("trial", "bank"), None, "zero"),
            P(("trial", "bank"), "zero"),
            P(("trial", "bank"), "zero"),
            P("trial", None),
        ),
        check_vma=False,
    )
```

time: 209 us -> 119 us (0.57)
  Pallas kernels: 0 us -> 115 us
  local copies, waits for them, and re-layouts: 76.9 us -> 1.34 us
  waiting for transfers between devices: 69.1 us -> 0 us
  starting transfers between devices: 42 us -> 0 us
  other arithmetic: 19 us -> 0 us
    pallas_call x0 -> x2, Pallas kernels: none -> 115 us  [the longest x1 112 us: local(): pl.pallas_call(spread_kernel, out_shape=(jax.ShapeDtypeStruct((PEERS, PAI...]
    all_to_all x6 -> x0, waiting for transfers between devices: 69.1 us -> none  [the longest x1 27.8 us: local(): lax.all_to_all(narrow_gate, 'zero', split_axis=2, concat_axis=1, tiled=True)]
    unnamed x14 -> x4, local copies, waits for them, and re-layouts: 45.5 us -> 1.34 us
    all_to_all x6 -> x0, starting transfers between devices: 42 us -> none  [the longest x3 15.3 us: sent_to_all(): lax.all_to_all(jnp.broadcast_to(array[None], (count, *array.shape)), axis...]
    all_to_all x6 -> x0, local copies, waits for them, and re-layouts: 28 us -> none  [the longest x2 13.6 us: local(): lax.all_to_all(narrow_up, 'zero', split_axis=2, concat_axis=1, tiled=True)]
    unnamed x2 -> x0, other arithmetic: 13.8 us -> none
    reduce_sum x2 -> x0, other arithmetic: 5.13 us -> none  [the longest x1 5.03 us: local(): jnp.sum(jnp.abs(w_up), axis=1)]
  transfers between devices with their start and end apart: 6 -> 0, of which waited for: 5 -> 0; matrix products, arithmetic and copies ran while one was open for 29% -> 0% of each run, Pallas kernels for 0% -> 0%
where the time goes in v1:
time: 119 us; the launch traced here: 117 us
  Pallas kernels  115 us (97%)
  local copies, waits for them, and re-layouts  1.34 us (1%)
    pallas_call x1, Pallas kernels, local(): pl.pallas_call(spread_kernel, out_shape=(jax.ShapeDtypeStruct((PEERS, PAI...  112 us
    pallas_call x1, Pallas kernels, local(): pl.pallas_call(place_kernel, out_shape=(jax.ShapeDtypeStruct((16, COLS, D...  3.07 us

profile of v1, /device:TPU:10, one launch (start us, length us, event | category | flops | bytes accessed | tf_op | source)
XLA Modules:
  0.0 117.4 jit_solution(18229951768957534529)
XLA Ops:
  0.6 0.0 copy-start
  0.6 0.7 copy-done
  1.3 0.0 copy-start.1
  1.3 0.7 copy-done.1
  2.0 112.4 %shard_map.83 = (bf16[32,16,32,128]{3,2,1,0:T(8,128)(2,1)S(1)}, f32[8,128]{1,0:T(8,128)S(1)}, bf16[4,16,2048]{2,1,0:T(8,128)(2,1)S(1)}) custom-call(f32[16,64,1024]{2,1,0:T(8,128)} %gate.1, f32[16,64,1024]{2,1,0:T(8,128)} %up.1, f32[16,64]{1,0:T(8,128)S(1)} %bitcast.7, f32[1,64]{1,0:T(1,128)S(1)} %bitcast.8), custom_call_target="tpu_custom_call" | custom-call | tf_op jit(solution)/shard_map/pallas_call | solution.py:206
  114.4 3.1 %shard_map.84 = (bf16[16,32,2048]{2,1,0:T(8,128)(2,1)}, bf16[16,32,2048]{2,1,0:T(8,128)(2,1)}, f32[16,32]{1,0:T(8,128)}, f32[16,32]{1,0:T(8,128)}, bf16[4,16,2048]{2,1,0:T(8,128)(2,1)}) custom-call(bf16[32,16,32,128]{3,2,1,0:T(8,128)(2,1)S(1)} %get-tuple-element.13.rx, f32[8,128]{1,0:T(8,128)S(1)} %get-tuple-element.14.scales, ...), custom_call_target="tpu_custom_call" | custom-call | tf_op jit(solution)/shard_map/pallas_call | solution.py:235
Async XLA Ops:
  0.6 0.7 copy-start
  1.3 0.7 copy-start.1

commit v2 on v1

v2 whole, which is shorter than its diff:
```python
import jax
import jax.numpy as jnp
from jax import lax
from jax.experimental import pallas as pl
from jax.experimental.pallas import tpu as pltpu
from jax.sharding import PartitionSpec as P

MESH = pl.DeviceIdType.MESH
D_MODEL = 2048
PEERS = 32
BANKS = 4
MATS = 32
BLOCKS = ((0, 0), (1, 0), (0, 4), (0, 8), (0, 12), (1, 4), (1, 8), (1, 12))
PAIRS = MATS // 2
COLS = 32
CHUNKS = ((0, 1), (1, 1), (2, 2), (4, 1), (5, 1), (6, 2), (8, 4), (12, 3), (15, 1))
CODED = 4
POWER = 13
TOP = 2.0**9
LEAST = 1e-30
LOADS = 8


def far_first(k, me):
    t, u = k // 4, lax.rem(k, 4)
    dz = 4 + (2 * lax.rem(t, 2) - 1) * ((t + 1) // 2)
    dy = 2 + (2 * lax.rem(u, 2) - 1) * ((u + 1) // 2)
    z, y = me // 4, lax.rem(me, 4)
    return lax.rem(z + dz, 8) * 4 + lax.rem(y + dy, 4)


def joined(left, right):
    left, right = left.astype(jnp.float32), right.astype(jnp.float32)
    return (
        jnp.concatenate([left[:, :64], right[:, :64]], axis=1),
        jnp.concatenate([left[:, 64:], right[:, 64:]], axis=1),
    )


def tile_of(block, factor):
    return (block * factor[:, None, :]).reshape(128, 128)


def decoded(tile, factor):
    v = tile.astype(jnp.float32)
    size = jnp.exp(jnp.log(jnp.abs(v)) * (1.0 / POWER)) * factor
    return jnp.where(v == 0.0, 0.0, jnp.where(v < 0.0, -size, size))


def spread_kernel(
    gate, up, router, gain,
    placed, scale_gate, scale_up, router_out,
    w, rs_tx, rs_rx, ag_tx, ag_z, ag_y, turned, tx, rx, rt_in, gain_in, rt_tx, rt_z, rt_y,
    load_sem, rs_send, rs_recv, az_send, az_recv, ay_send, ay_recv,
    z_send, z_recv, y_send, y_recv,
    x_send, x_recv, send, recv,
):
    me, bank = lax.axis_index("zero"), lax.axis_index("bank")
    z, y = me // 4, lax.rem(me, 4)

    per = MATS // LOADS
    loads = []
    for n, (which, first) in enumerate(BLOCKS):
        copy = pltpu.make_async_copy(
            (gate, up)[which].at[pl.ds(first, per)], w.at[pl.ds(n * per, per)], load_sem.at[n]
        )
        copy.start()
        loads.append(copy)

    small = []
    for n, (source, target) in enumerate(((router, rt_in), (gain, gain_in))):
        copy = pltpu.make_async_copy(source, target, load_sem.at[LOADS + n])
        copy.start()
        small.append(copy)

    barrier = pltpu.get_barrier_semaphore()

    @pl.loop(0, PEERS - 1)
    def _(k):
        pl.semaphore_signal(
            barrier, inc=1, device_id={"zero": far_first(k, me)}, device_id_type=MESH
        )

    for hop in range(1, BANKS):
        pl.semaphore_signal(
            barrier, inc=1, device_id={"bank": lax.rem(bank + hop, BANKS)}, device_id_type=MESH
        )

    lane = lax.broadcasted_iota(jnp.int32, (8, 128), 1) // 32

    def encode(p, sums):
        own = TOP / jnp.maximum(sums, LEAST)
        for q in range(8):
            here = slice(128 * q, 128 * q + 128)
            x = tile_of(w[2 * p : 2 * p + 2, :, here], own[:, here])
            x2 = x * x
            x4 = x2 * x2
            x12 = (x4 * x4) * x4
            tx[4 * q : 4 * q + 4, p] = (x12 * x).T.astype(jnp.bfloat16).reshape(4, COLS, 128)

    def sums_of(n):
        loads[n].wait()
        return jnp.sum(jnp.abs(w[n * per : (n + 1) * per]), axis=1)

    def to_zero(peer, src, dst, send_sem, recv_sem):
        pltpu.make_async_remote_copy(
            src_ref=src, dst_ref=dst, send_sem=send_sem, recv_sem=recv_sem,
            device_id={"zero": peer}, device_id_type=MESH,
        ).start()

    def to_peer(k, src, dst, send_sem, recv_sem):
        peer = far_first(k, me)
        to_zero(peer, src(peer), dst, send_sem, recv_sem)

    def bytes_of(ref, sem):
        pltpu.make_async_copy(ref, ref, sem).wait()

    others = pl.ds(0, PEERS - 1)

    def send_chunk(c):
        first, count = CHUNKS[c]
        span = pl.ds(first, count)

        @pl.loop(0, PEERS - 1)
        def _(k):
            to_peer(
                k, lambda peer: tx.at[peer, span], rx.at[me, span], send.at[c], recv.at[c]
            )

        rx[me, first : first + count] = tx[me, first : first + count]

    parts = [sums_of(0)]
    encode(0, parts[0][:2])
    pl.semaphore_wait(barrier, PEERS - 1 + BANKS - 1)
    send_chunk(0)

    for n in range(1, LOADS):
        parts.append(sums_of(n))
    sums = jnp.concatenate(parts, axis=0)
    for q in range(8):
        blocks = [sums[8 * a : 8 * a + 8, 128 * q : 128 * q + 128] for a in range(4)]
        for r in range(4):
            tile = None
            for a in range(4):
                moved = pltpu.roll(blocks[a], (32 * (a - r)) % 128, 1) if a != r else blocks[a]
                tile = moved if tile is None else jnp.where(lane == a, moved, tile)
            rs_tx[4 * q + r] = tile

    @pl.loop(0, PEERS - 1)
    def _(k):
        to_peer(k, lambda peer: rs_tx.at[peer], rs_rx.at[me], rs_send, rs_recv)

    encode(1, parts[0][2:])
    send_chunk(1)

    for copy in small:
        copy.wait()
    made = rt_in[...] * gain_in[...]
    rt_tx[...] = jnp.concatenate([made[:8], made[8:]], axis=1).astype(jnp.bfloat16)

    for hop in (4, 3, 5, 2, 6, 1, 7):
        to_zero(lax.rem(z + hop, 8) * 4 + y, rt_tx, rt_z.at[z], z_send, z_recv)

    rs_rx[me] = rs_tx[me]
    rt_z[z] = rt_tx[...]
    for p in range(2, CODED):
        encode(p, parts[1][2 * p - 4 : 2 * p - 2])

    bytes_of(rs_rx.at[others], rs_recv)
    scale = jnp.sum(rs_rx[...], axis=0) / D_MODEL
    for n, (which, first) in enumerate(BLOCKS):
        target = (scale_gate, scale_up)[which]
        target[first : first + per] = scale[
            n * per % 8 : n * per % 8 + per, n // 2 * COLS : n // 2 * COLS + COLS
        ]
    ag_tx[...] = 1.0 / scale

    for hop in (4, 3, 5, 2, 6, 1, 7):
        to_zero(lax.rem(z + hop, 8) * 4 + y, ag_tx, ag_z.at[z], az_send, az_recv)
    ag_z[z] = ag_tx[...]

    send_chunk(2)

    bytes_of(rt_z.at[pl.ds(0, 7)], z_recv)
    for hop in (2, 1, 3):
        to_zero(z * 4 + lax.rem(y + hop, 4), rt_z, rt_y.at[y], y_send, y_recv)
    rt_y[y] = rt_z[...]

    bytes_of(ag_z.at[pl.ds(0, 7)], az_recv)
    for hop in (2, 1, 3):
        to_zero(z * 4 + lax.rem(y + hop, 4), ag_z, ag_y.at[y], ay_send, ay_recv)
    ag_y[y] = ag_z[...]

    back = (1.0 / TOP) / scale
    for k in range(PEERS):
        turned[k] = (jnp.maximum(rs_rx[k], LEAST) * back).T[:COLS]

    bytes_of(ag_y.at[pl.ds(0, 3)], ay_recv)
    rows = []
    for a in range(1, 4):
        along = []
        for q in range(8):
            block = None
            for r in range(4):
                tile = ag_y[r, q]
                moved = pltpu.roll(tile, (32 * (r - a)) % 128, 1) if a != r else tile
                block = moved if block is None else jnp.where(lane == r, moved, block)
            along.append(block)
        rows.append(along)

    for c in range(3, len(CHUNKS)):
        first, count = CHUNKS[c]
        for p in range(first, first + count):
            for q in range(8):
                g = 2 * p
                x = tile_of(
                    w[g : g + 2, :, 128 * q : 128 * q + 128], rows[g // 8 - 1][q][g % 8 : g % 8 + 2]
                )
                tx[4 * q : 4 * q + 4, p] = x.T.astype(jnp.bfloat16).reshape(4, COLS, 128)
        send_chunk(c)

    bytes_of(rt_y.at[pl.ds(0, 3)], y_recv)
    for k in range(PEERS // 2):
        low, high = joined(rt_y[2 * (k % 2), k // 2], rt_y[2 * (k % 2) + 1, k // 2])
        router_out[bank, :, 128 * k : 128 * k + 128] = jnp.concatenate([low, high], axis=0).astype(
            jnp.bfloat16
        )
    crossing = []
    half = lax.broadcasted_iota(jnp.int32, (COLS, 128), 1) < 64
    for hop in range(1, BANKS):
        copy = pltpu.make_async_remote_copy(
            src_ref=router_out.at[bank], dst_ref=router_out.at[bank],
            send_sem=x_send.at[hop - 1], recv_sem=x_recv.at[hop - 1],
            device_id={"bank": lax.rem(bank + hop, BANKS)}, device_id_type=MESH,
        )
        copy.start()
        crossing.append(copy)

    for c, (first, count) in enumerate(CHUNKS):
        bytes_of(rx.at[others, pl.ds(first, count)], recv.at[c])
        for p in range(first, first + count):
            for k in range(PEERS // 2):
                pair = []
                for n in (2 * k, 2 * k + 1):
                    tile = rx[n, p]
                    if p < CODED:
                        both = turned[n]
                        factor = jnp.where(
                            half, both[:, 2 * p : 2 * p + 1], both[:, 2 * p + 1 : 2 * p + 2]
                        )
                        tile = decoded(tile, factor)
                    pair.append(tile)
                even, odd = joined(*pair)
                here = slice(128 * k, 128 * k + 128)
                placed[2 * p, :, here] = even.astype(jnp.bfloat16)
                placed[2 * p + 1, :, here] = odd.astype(jnp.bfloat16)

    for copy in crossing:
        copy.wait()
    bytes_of(rs_rx.at[others], rs_send)
    bytes_of(ag_z.at[pl.ds(0, 7)], az_send)
    bytes_of(ag_y.at[pl.ds(0, 3)], ay_send)
    bytes_of(rt_z.at[pl.ds(0, 7)], z_send)
    bytes_of(rt_y.at[pl.ds(0, 3)], y_send)
    for c, (first, count) in enumerate(CHUNKS):
        bytes_of(tx.at[others, pl.ds(first, count)], send.at[c])


def store_kernel(placed, scale_gate, scale_up, router, *out):
    gate_out, up_out, scale_gate_out, scale_up_out, router_out, sem = out
    per = MATS // LOADS
    moves = [(scale_gate, scale_gate_out), (scale_up, scale_up_out)]
    for n, (which, first) in enumerate(BLOCKS):
        target = (gate_out, up_out)[which]
        moves.append((placed.at[pl.ds(n * per, per)], target.at[pl.ds(first, per)]))
    moves.append((router, router_out))
    copies = [pltpu.make_async_copy(a, b, sem.at[n]) for n, (a, b) in enumerate(moves)]
    for copy in copies:
        copy.start()
    for copy in copies:
        copy.wait()


def local(w_gate, w_up, router_weight, router_gain):
    f32, bf16 = jnp.float32, jnp.bfloat16
    vmem, anywhere = pl.BlockSpec(memory_space=pltpu.VMEM), pl.BlockSpec(memory_space=pl.ANY)
    dma = pltpu.SemaphoreType.DMA
    given = (w_gate, w_up, router_weight.T, router_gain.reshape(1, -1))
    served = jax.ShapeDtypeStruct((16, COLS, D_MODEL), bf16)
    scale = jax.ShapeDtypeStruct((16, COLS), f32)
    router = jax.ShapeDtypeStruct((BANKS, 16, D_MODEL), bf16)
    arrived = pl.pallas_call(
        spread_kernel,
        out_shape=(jax.ShapeDtypeStruct((MATS, COLS, D_MODEL), bf16), scale, scale, router),
        in_specs=[anywhere] * 4,
        out_specs=(vmem,) * 4,
        scratch_shapes=[
            pltpu.VMEM((MATS, 64, 1024), f32),
            pltpu.VMEM((PEERS, 8, 128), f32),
            pltpu.VMEM((PEERS, 8, 128), f32),
            pltpu.VMEM((8, 128), f32),
            pltpu.VMEM((8, 8, 128), f32),
            pltpu.VMEM((4, 8, 8, 128), f32),
            pltpu.VMEM((PEERS, COLS, 8), f32),
            pltpu.VMEM((PEERS, PAIRS, COLS, 128), bf16),
            pltpu.VMEM((PEERS, PAIRS, COLS, 128), bf16),
            pltpu.VMEM((16, 64), f32),
            pltpu.VMEM((1, 64), f32),
            pltpu.VMEM((8, 128), bf16),
            pltpu.VMEM((8, 8, 128), bf16),
            pltpu.VMEM((4, 8, 8, 128), bf16),
            dma((LOADS + 2,)),
            *[dma(())] * 10,
            dma((BANKS - 1,)),
            dma((BANKS - 1,)),
            dma((len(CHUNKS),)),
            dma((len(CHUNKS),)),
        ],
        compiler_params=pltpu.CompilerParams(
            collective_id=0, has_side_effects=True, vmem_limit_bytes=46 * 2**20
        ),
    )(*[pltpu.with_memory_space_constraint(a, pltpu.HBM) for a in given])
    serve_gate, serve_up, scale_gate, scale_up, router = pl.pallas_call(
        store_kernel,
        out_shape=(served, served, scale, scale, router),
        in_specs=[vmem] * 4,
        out_specs=(anywhere,) * 5,
        scratch_shapes=[dma((11,))],
        compiler_params=pltpu.CompilerParams(vmem_limit_bytes=32 * 2**20),
    )(*arrived)
    return (
        jnp.swapaxes(serve_gate, 1, 2),
        jnp.swapaxes(serve_up, 1, 2),
        scale_gate,
        scale_up,
        router.reshape(BANKS * 16, D_MODEL).T,
    )


def solution(mesh):
    placed = (
        P(("trial", "bank"), "zero", None),
        P(("trial", "bank"), "zero", None),
        P(("trial", "zero"), "bank"),
        P(("trial", "zero")),
    )
    return jax.shard_map(
        local,
        mesh=mesh,
        in_specs=placed,
        out_specs=(
            P(("trial", "bank"), None, "zero"),
            P(("trial", "bank"), None, "zero"),
            P(("trial", "bank"), "zero"),
            P(("trial", "bank"), "zero"),
            P("trial", None),
        ),
        check_vma=False,
    )
```

time: 119 us -> 110 us (0.924)
  Pallas kernels: 115 us -> 108 us
  local copies, waits for them, and re-layouts: 1.34 us -> 0 us
    pallas_call x2, Pallas kernels: 115 us -> 108 us  [the longest x1 105 us: local(): pl.pallas_call(spread_kernel, out_shape=(jax.ShapeDtypeStruct((MATS, COLS...]
    unnamed x4 -> x0, local copies, waits for them, and re-layouts: 1.34 us -> none
where the time goes in v2:
time: 110 us; the launch traced here: 108 us
  Pallas kernels  108 us (98%)
    pallas_call x1, Pallas kernels, local(): pl.pallas_call(spread_kernel, out_shape=(jax.ShapeDtypeStruct((MATS, COLS...  105 us

profile of v2, /device:TPU:10, one launch (start us, length us, event | category | flops | bytes accessed | tf_op | source)
XLA Modules:
  0.0 108.3 jit_solution(6319869062576301192)
XLA Ops:
  0.6 105.5 %shard_map.83 = (bf16[32,32,2048]{2,1,0:T(8,128)(2,1)S(1)}, f32[16,32]{1,0:T(8,128)S(1)}, f32[16,32]{1,0:T(8,128)S(1)}, bf16[4,16,2048]{2,1,0:T(8,128)(2,1)S(1)}) custom-call(f32[16,64,1024]{2,1,0:T(8,128)} %gate.1, f32[16,64,1024]{2,1,0:T(8,128)} %up.1, f32[16,64]{1,0:T(8,128)} %bitcast.7, f32[1,64]{1,0:T(1,128)} %bitcast.8), custom_call_target="tpu_custom_call" | custom-call | tf_op jit(solution)/shard_map/pallas_call | solution.py:292
  106.1 2.2 %shard_map.84 = (bf16[16,32,2048]{2,1,0:T(8,128)(2,1)}, bf16[16,32,2048]{2,1,0:T(8,128)(2,1)}, f32[16,32]{1,0:T(8,128)}, f32[16,32]{1,0:T(8,128)}, bf16[4,16,2048]{2,1,0:T(8,128)(2,1)}) custom-call(bf16[32,32,2048]{2,1,0:T(8,128)(2,1)S(1)} %get-tuple-element.14.placed, f32[16,32]{1,0:T(8,128)S(1)} %get-tuple-element.15.scale_gate, ...), custom_call_target="tpu_custom_call" | custom-call | tf_op jit(solution)/shard_map/pallas_call | solution.py:323

commit v3 on v2

--- a/solution.py
+++ b/solution.py
@@ -10,15 +10,17 @@
 PEERS = 32
 BANKS = 4
 MATS = 32
-BLOCKS = ((0, 0), (1, 0), (0, 4), (0, 8), (0, 12), (1, 4), (1, 8), (1, 12))
 PAIRS = MATS // 2
 COLS = 32
-CHUNKS = ((0, 1), (1, 1), (2, 2), (4, 1), (5, 1), (6, 2), (8, 4), (12, 3), (15, 1))
-CODED = 4
+BLOCKS = ((0, 0), (1, 0), (0, 2), (1, 2), (0, 4)) + tuple(
+    [(0, e) for e in range(6, 16, 2)] + [(1, e) for e in range(4, 16, 2)]
+)
+CHUNKS = ((0, 1), (1, 1), (2, 1), (3, 1), (4, 1), (5, 1), (6, 2), (8, 4), (12, 3), (15, 1))
+CODED = 5
 POWER = 13
 TOP = 2.0**9
 LEAST = 1e-30
-LOADS = 8
+Z_HOPS, Y_HOPS = (4, 3, 5, 2, 6, 1, 7), (2, 1, 3)
 
 
 def far_first(k, me):
@@ -50,26 +52,23 @@
 def spread_kernel(
     gate, up, router, gain,
     placed, scale_gate, scale_up, router_out,
-    w, rs_tx, rs_rx, ag_tx, ag_z, ag_y, turned, tx, rx, rt_in, gain_in, rt_tx, rt_z, rt_y,
-    load_sem, rs_send, rs_recv, az_send, az_recv, ay_send, ay_recv,
-    z_send, z_recv, y_send, y_recv,
-    x_send, x_recv, send, recv,
+    w, rs_tx, rs_y, rs_zt, rs_z, nm_tx, nm_z, nm_y, nm_t, ag_tx, ag_z, ag_y, turned, tx, rx,
+    rt_in, gain_in, rt_tx, rt_z, rt_y,
+    load_sem, stage_send, stage_recv, x_send, x_recv, send, recv,
 ):
     me, bank = lax.axis_index("zero"), lax.axis_index("bank")
     z, y = me // 4, lax.rem(me, 4)
 
-    per = MATS // LOADS
     loads = []
     for n, (which, first) in enumerate(BLOCKS):
         copy = pltpu.make_async_copy(
-            (gate, up)[which].at[pl.ds(first, per)], w.at[pl.ds(n * per, per)], load_sem.at[n]
+            (gate, up)[which].at[pl.ds(first, 2)], w.at[pl.ds(2 * n, 2)], load_sem.at[n]
         )
         copy.start()
         loads.append(copy)
-
     small = []
     for n, (source, target) in enumerate(((router, rt_in), (gain, gain_in))):
-        copy = pltpu.make_async_copy(source, target, load_sem.at[LOADS + n])
+        copy = pltpu.make_async_copy(source, target, load_sem.at[PAIRS + n])
         copy.start()
         small.append(copy)
 
@@ -88,8 +87,9 @@
 
     lane = lax.broadcasted_iota(jnp.int32, (8, 128), 1) // 32
 
-    def encode(p, sums):
-        own = TOP / jnp.maximum(sums, LEAST)
+    def encode(p):
+        norm = jnp.maximum(norms[p].astype(jnp.float32), LEAST)
+        own = TOP / norm
         for q in range(8):
             here = slice(128 * q, 128 * q + 128)
             x = tile_of(w[2 * p : 2 * p + 2, :, here], own[:, here])
@@ -100,7 +100,7 @@
 
     def sums_of(n):
         loads[n].wait()
-        return jnp.sum(jnp.abs(w[n * per : (n + 1) * per]), axis=1)
+        return jnp.sum(jnp.abs(w[2 * n : 2 * n + 2]), axis=1)
 
     def to_zero(peer, src, dst, send_sem, recv_sem):
         pltpu.make_async_remote_copy(
@@ -117,6 +117,22 @@
 
     others = pl.ds(0, PEERS - 1)
 
+    def along_z(n, src, dst):
+        for hop in Z_HOPS:
+            there = lax.rem(z + hop, 8)
+            to_zero(there * 4 + y, src(there), dst.at[z], stage_send.at[n], stage_recv.at[n])
+
+    def along_y(n, src, dst):
+        for hop in Y_HOPS:
+            there = lax.rem(y + hop, 4)
+            to_zero(z * 4 + there, src(there), dst.at[y], stage_send.at[n], stage_recv.at[n])
+
+    def arrived_z(n, dst):
+        bytes_of(dst.at[pl.ds(0, 7)], stage_recv.at[n])
+
+    def arrived_y(n, dst):
+        bytes_of(dst.at[pl.ds(0, 3)], stage_recv.at[n])
+
     def send_chunk(c):
         first, count = CHUNKS[c]
         span = pl.ds(first, count)
@@ -130,74 +146,75 @@
         rx[me, first : first + count] = tx[me, first : first + count]
 
     parts = [sums_of(0)]
-    encode(0, parts[0][:2])
+    norms = [parts[0].astype(jnp.bfloat16)]
+    encode(0)
     pl.semaphore_wait(barrier, PEERS - 1 + BANKS - 1)
     send_chunk(0)
 
-    for n in range(1, LOADS):
+    for n in range(1, PAIRS):
         parts.append(sums_of(n))
+    norms += [parts[n].astype(jnp.bfloat16) for n in range(1, CODED)]
     sums = jnp.concatenate(parts, axis=0)
     for q in range(8):
         blocks = [sums[8 * a : 8 * a + 8, 128 * q : 128 * q + 128] for a in range(4)]
+        nm_tx[q] = jnp.concatenate(blocks[:2], axis=0).astype(jnp.bfloat16)
         for r in range(4):
             tile = None
             for a in range(4):
                 moved = pltpu.roll(blocks[a], (32 * (a - r)) % 128, 1) if a != r else blocks[a]
                 tile = moved if tile is None else jnp.where(lane == a, moved, tile)
-            rs_tx[4 * q + r] = tile
-
-    @pl.loop(0, PEERS - 1)
-    def _(k):
-        to_peer(k, lambda peer: rs_tx.at[peer], rs_rx.at[me], rs_send, rs_recv)
-
-    encode(1, parts[0][2:])
+            rs_tx[r, q] = tile
+    along_y(0, lambda there: rs_tx.at[there], rs_y)
+    rs_y[y] = rs_tx[y]
+
+    encode(1)
     send_chunk(1)
 
     for copy in small:
         copy.wait()
     made = rt_in[...] * gain_in[...]
     rt_tx[...] = jnp.concatenate([made[:8], made[8:]], axis=1).astype(jnp.bfloat16)
-
-    for hop in (4, 3, 5, 2, 6, 1, 7):
-        to_zero(lax.rem(z + hop, 8) * 4 + y, rt_tx, rt_z.at[z], z_send, z_recv)
-
-    rs_rx[me] = rs_tx[me]
+    along_z(1, lambda there: nm_tx.at[there], nm_z)
+    along_z(2, lambda there: rt_tx, rt_z)
+    nm_z[z] = nm_tx[z]
     rt_z[z] = rt_tx[...]
-    for p in range(2, CODED):
-        encode(p, parts[1][2 * p - 4 : 2 * p - 2])
-
-    bytes_of(rs_rx.at[others], rs_recv)
-    scale = jnp.sum(rs_rx[...], axis=0) / D_MODEL
+    encode(2)
+
+    arrived_y(0, rs_y)
+    rs_zt[...] = jnp.sum(rs_y[...], axis=0)
+    along_z(3, lambda there: rs_zt.at[there], rs_z)
+    rs_z[z] = rs_zt[z]
+    send_chunk(2)
+    encode(3)
+
+    arrived_z(3, rs_z)
+    scale = jnp.sum(rs_z[...], axis=0) / D_MODEL
+    ag_tx[...] = 1.0 / scale
+    along_z(4, lambda there: ag_tx, ag_z)
+    ag_z[z] = ag_tx[...]
+    send_chunk(3)
+    encode(4)
+
     for n, (which, first) in enumerate(BLOCKS):
         target = (scale_gate, scale_up)[which]
-        target[first : first + per] = scale[
-            n * per % 8 : n * per % 8 + per, n // 2 * COLS : n // 2 * COLS + COLS
+        target[first : first + 2] = scale[
+            2 * n % 8 : 2 * n % 8 + 2, n // 4 * COLS : n // 4 * COLS + COLS
         ]
-    ag_tx[...] = 1.0 / scale
-
-    for hop in (4, 3, 5, 2, 6, 1, 7):
-        to_zero(lax.rem(z + hop, 8) * 4 + y, ag_tx, ag_z.at[z], az_send, az_recv)
-    ag_z[z] = ag_tx[...]
-
-    send_chunk(2)
-
-    bytes_of(rt_z.at[pl.ds(0, 7)], z_recv)
-    for hop in (2, 1, 3):
-        to_zero(z * 4 + lax.rem(y + hop, 4), rt_z, rt_y.at[y], y_send, y_recv)
+    arrived_z(1, nm_z)
+    along_y(5, lambda there: nm_z, nm_y)
+    nm_y[y] = nm_z[...]
+    arrived_z(2, rt_z)
+    along_y(6, lambda there: rt_z, rt_y)
     rt_y[y] = rt_z[...]
 
-    bytes_of(ag_z.at[pl.ds(0, 7)], az_recv)
-    for hop in (2, 1, 3):
-        to_zero(z * 4 + lax.rem(y + hop, 4), ag_z, ag_y.at[y], ay_send, ay_recv)
+    arrived_z(4, ag_z)
+    along_y(7, lambda there: ag_z, ag_y)
     ag_y[y] = ag_z[...]
-
-    back = (1.0 / TOP) / scale
-    for k in range(PEERS):
-        turned[k] = (jnp.maximum(rs_rx[k], LEAST) * back).T[:COLS]
-
-    bytes_of(ag_y.at[pl.ds(0, 3)], ay_recv)
+    send_chunk(4)
+
+    arrived_y(7, ag_y)
     rows = []
-    for a in range(1, 4):
+    for a in range(CODED // 4, 4):
         along = []
         for q in range(8):
             block = None
@@ -208,18 +225,28 @@
             along.append(block)
         rows.append(along)
 
-    for c in range(3, len(CHUNKS)):
+    for c in range(CODED, len(CHUNKS)):
         first, count = CHUNKS[c]
         for p in range(first, first + count):
             for q in range(8):
                 g = 2 * p
                 x = tile_of(
-                    w[g : g + 2, :, 128 * q : 128 * q + 128], rows[g // 8 - 1][q][g % 8 : g % 8 + 2]
+                    w[g : g + 2, :, 128 * q : 128 * q + 128],
+                    rows[g // 8 - CODED // 4][q][g % 8 : g % 8 + 2],
                 )
                 tx[4 * q : 4 * q + 4, p] = x.T.astype(jnp.bfloat16).reshape(4, COLS, 128)
         send_chunk(c)
 
-    bytes_of(rt_y.at[pl.ds(0, 3)], y_recv)
+    back = ((1.0 / TOP) / scale).T
+    back = jnp.concatenate([back[:COLS], back[COLS : 2 * COLS]], axis=1)
+    arrived_y(5, nm_y)
+    for k in range(PEERS):
+        nm_t[k] = jnp.maximum(nm_y[k % 4, k // 4].astype(jnp.float32), LEAST).T
+    mine = pl.ds(pl.multiple_of(COLS * y, COLS), COLS)
+    for k in range(PEERS):
+        turned[k] = nm_t[k, mine] * back
+
+    arrived_y(6, rt_y)
     for k in range(PEERS // 2):
         low, high = joined(rt_y[2 * (k % 2), k // 2], rt_y[2 * (k % 2) + 1, k // 2])
         router_out[bank, :, 128 * k : 128 * k + 128] = jnp.concatenate([low, high], axis=0).astype(
@@ -257,22 +284,24 @@
 
     for copy in crossing:
         copy.wait()
-    bytes_of(rs_rx.at[others], rs_send)
-    bytes_of(ag_z.at[pl.ds(0, 7)], az_send)
-    bytes_of(ag_y.at[pl.ds(0, 3)], ay_send)
-    bytes_of(rt_z.at[pl.ds(0, 7)], z_send)
-    bytes_of(rt_y.at[pl.ds(0, 3)], y_send)
+    for n, sent in enumerate((rs_y, nm_z, rt_z, rs_z, ag_z, nm_y, rt_y, ag_y)):
+        bytes_of(sent.at[pl.ds(0, sent.shape[0] - 1)], stage_send.at[n])
     for c, (first, count) in enumerate(CHUNKS):
         bytes_of(tx.at[others, pl.ds(first, count)], send.at[c])
 
 
 def store_kernel(placed, scale_gate, scale_up, router, *out):
     gate_out, up_out, scale_gate_out, scale_up_out, router_out, sem = out
-    per = MATS // LOADS
     moves = [(scale_gate, scale_gate_out), (scale_up, scale_up_out)]
+    runs = []
     for n, (which, first) in enumerate(BLOCKS):
+        if runs and runs[-1][0] == which and runs[-1][1] + runs[-1][3] == first:
+            runs[-1][3] += 2
+        else:
+            runs.append([which, first, 2 * n, 2])
+    for which, first, at, count in runs:
         target = (gate_out, up_out)[which]
-        moves.append((placed.at[pl.ds(n * per, per)], target.at[pl.ds(first, per)]))
+        moves.append((placed.at[pl.ds(at, count)], target.at[pl.ds(first, count)]))
     moves.append((router, router_out))
     copies = [pltpu.make_async_copy(a, b, sem.at[n]) for n, (a, b) in enumerate(moves)]
     for copy in copies:
@@ -296,12 +325,18 @@
         out_specs=(vmem,) * 4,
         scratch_shapes=[
             pltpu.VMEM((MATS, 64, 1024), f32),
-            pltpu.VMEM((PEERS, 8, 128), f32),
-            pltpu.VMEM((PEERS, 8, 128), f32),
+            pltpu.VMEM((4, 8, 8, 128), f32),
+            pltpu.VMEM((4, 8, 8, 128), f32),
+            pltpu.VMEM((8, 8, 128), f32),
+            pltpu.VMEM((8, 8, 128), f32),
+            pltpu.VMEM((8, 16, 128), bf16),
+            pltpu.VMEM((8, 16, 128), bf16),
+            pltpu.VMEM((4, 8, 16, 128), bf16),
+            pltpu.VMEM((PEERS, 128, 16), f32),
             pltpu.VMEM((8, 128), f32),
             pltpu.VMEM((8, 8, 128), f32),
             pltpu.VMEM((4, 8, 8, 128), f32),
-            pltpu.VMEM((PEERS, COLS, 8), f32),
+            pltpu.VMEM((PEERS, COLS, 16), f32),
             pltpu.VMEM((PEERS, PAIRS, COLS, 128), bf16),
             pltpu.VMEM((PEERS, PAIRS, COLS, 128), bf16),
             pltpu.VMEM((16, 64), f32),
@@ -309,8 +344,9 @@
             pltpu.VMEM((8, 128), bf16),
             pltpu.VMEM((8, 8, 128), bf16),
             pltpu.VMEM((4, 8, 8, 128), bf16),
-            dma((LOADS + 2,)),
-            *[dma(())] * 10,
+            dma((PAIRS + 2,)),
+            dma((8,)),
+            dma((8,)),
             dma((BANKS - 1,)),
             dma((BANKS - 1,)),
             dma((len(CHUNKS),)),
@@ -325,7 +361,7 @@
         out_shape=(served, served, scale, scale, router),
         in_specs=[vmem] * 4,
         out_specs=(anywhere,) * 5,
-        scratch_shapes=[dma((11,))],
+        scratch_shapes=[dma((16,))],
         compiler_params=pltpu.CompilerParams(vmem_limit_bytes=32 * 2**20),
     )(*arrived)
     return (

time: 110 us -> 109 us (level)
    pallas_call x1, Pallas kernels: 105 us -> 104 us  [local(): pl.pallas_call(spread_kernel, out_shape=(jax.ShapeDtypeStruct((MATS, COLS...]
where the time goes in v3:
time: 109 us; the launch traced here: 107 us
  Pallas kernels  107 us (98%)
    pallas_call x1, Pallas kernels, local(): pl.pallas_call(spread_kernel, out_shape=(jax.ShapeDtypeStruct((MATS, COLS...  104 us
    pallas_call x1, Pallas kernels, local(): pl.pallas_call(store_kernel, out_shape=(served, served, scale, scale, rou...  2.23 us

profile of v3, /device:TPU:10, one launch (start us, length us, event | category | flops | bytes accessed | tf_op | source)
XLA Modules:
  0.0 107.2 jit_solution(13303027046257012516)
XLA Ops:
  0.6 104.3 %shard_map.83 = (bf16[32,32,2048]{2,1,0:T(8,128)(2,1)S(1)}, f32[16,32]{1,0:T(8,128)S(1)}, f32[16,32]{1,0:T(8,128)S(1)}, bf16[4,16,2048]{2,1,0:T(8,128)(2,1)S(1)}) custom-call(f32[16,64,1024]{2,1,0:T(8,128)} %gate.1, f32[16,64,1024]{2,1,0:T(8,128)} %up.1, f32[16,64]{1,0:T(8,128)} %bitcast.7, f32[1,64]{1,0:T(1,128)} %bitcast.8), custom_call_target="tpu_custom_call" | custom-call | tf_op jit(solution)/shard_map/pallas_call | solution.py:321
  104.9 2.2 %shard_map.84 = (bf16[16,32,2048]{2,1,0:T(8,128)(2,1)}, bf16[16,32,2048]{2,1,0:T(8,128)(2,1)}, f32[16,32]{1,0:T(8,128)}, f32[16,32]{1,0:T(8,128)}, bf16[4,16,2048]{2,1,0:T(8,128)(2,1)}) custom-call(bf16[32,32,2048]{2,1,0:T(8,128)(2,1)S(1)} %get-tuple-element.14.placed, f32[16,32]{1,0:T(8,128)S(1)} %get-tuple-element.15.scale_gate, ...), custom_call_target="tpu_custom_call" | custom-call | tf_op jit(solution)/shard_map/pallas_call | solution.py:359

commit v4 on v3

--- a/solution.py
+++ b/solution.py
@@ -15,7 +15,7 @@
 BLOCKS = ((0, 0), (1, 0), (0, 2), (1, 2), (0, 4)) + tuple(
     [(0, e) for e in range(6, 16, 2)] + [(1, e) for e in range(4, 16, 2)]
 )
-CHUNKS = ((0, 1), (1, 1), (2, 1), (3, 1), (4, 1), (5, 1), (6, 2), (8, 4), (12, 3), (15, 1))
+CHUNKS = ((0, 1), (1, 1), (2, 1), (3, 1), (4, 1), (5, 1), (6, 2), (8, 3), (11, 3), (14, 1), (15, 1))
 CODED = 5
 POWER = 13
 TOP = 2.0**9
@@ -23,12 +23,15 @@
 Z_HOPS, Y_HOPS = (4, 3, 5, 2, 6, 1, 7), (2, 1, 3)
 
 
+HOPS = sorted(
+    ((dz, dy) for dz in range(8) for dy in range(4) if (dz, dy) != (0, 0)),
+    key=lambda hop: (-min(hop[0], 8 - hop[0]) - min(hop[1], 4 - hop[1]), hop),
+)
+
+
 def far_first(k, me):
-    t, u = k // 4, lax.rem(k, 4)
-    dz = 4 + (2 * lax.rem(t, 2) - 1) * ((t + 1) // 2)
-    dy = 2 + (2 * lax.rem(u, 2) - 1) * ((u + 1) // 2)
-    z, y = me // 4, lax.rem(me, 4)
-    return lax.rem(z + dz, 8) * 4 + lax.rem(y + dy, 4)
+    dz, dy = HOPS[k]
+    return lax.rem(me // 4 + dz, 8) * 4 + lax.rem(lax.rem(me, 4) + dy, 4)
 
 
 def joined(left, right):
@@ -74,8 +77,7 @@
 
     barrier = pltpu.get_barrier_semaphore()
 
-    @pl.loop(0, PEERS - 1)
-    def _(k):
+    for k in range(PEERS - 1):
         pl.semaphore_signal(
             barrier, inc=1, device_id={"zero": far_first(k, me)}, device_id_type=MESH
         )
@@ -137,8 +139,7 @@
         first, count = CHUNKS[c]
         span = pl.ds(first, count)
 
-        @pl.loop(0, PEERS - 1)
-        def _(k):
+        for k in range(PEERS - 1):
             to_peer(
                 k, lambda peer: tx.at[peer, span], rx.at[me, span], send.at[c], recv.at[c]
             )

time: 109 us -> 108 us (level)
  no operation moved by 1% of the time
where the time goes in v4:
time: 108 us; the launch traced here: 107 us
  Pallas kernels  106 us (98%)
    pallas_call x1, Pallas kernels, local(): pl.pallas_call(spread_kernel, out_shape=(jax.ShapeDtypeStruct((MATS, COLS...  104 us
    pallas_call x1, Pallas kernels, local(): pl.pallas_call(store_kernel, out_shape=(served, served, scale, scale, rou...  2.23 us

profile of v4, /device:TPU:10, one launch (start us, length us, event | category | flops | bytes accessed | tf_op | source)
XLA Modules:
  0.0 106.9 jit_solution(425463720910627317)
XLA Ops:
  0.6 104.0 %shard_map.83 = (bf16[32,32,2048]{2,1,0:T(8,128)(2,1)S(1)}, f32[16,32]{1,0:T(8,128)S(1)}, f32[16,32]{1,0:T(8,128)S(1)}, bf16[4,16,2048]{2,1,0:T(8,128)(2,1)S(1)}) custom-call(f32[16,64,1024]{2,1,0:T(8,128)} %gate.1, f32[16,64,1024]{2,1,0:T(8,128)} %up.1, f32[16,64]{1,0:T(8,128)} %bitcast.7, f32[1,64]{1,0:T(1,128)} %bitcast.8), custom_call_target="tpu_custom_call" | custom-call | tf_op jit(solution)/shard_map/pallas_call | solution.py:322
  104.6 2.2 %shard_map.84 = (bf16[16,32,2048]{2,1,0:T(8,128)(2,1)}, bf16[16,32,2048]{2,1,0:T(8,128)(2,1)}, f32[16,32]{1,0:T(8,128)}, f32[16,32]{1,0:T(8,128)}, bf16[4,16,2048]{2,1,0:T(8,128)(2,1)}) custom-call(bf16[32,32,2048]{2,1,0:T(8,128)(2,1)S(1)} %get-tuple-element.14.placed, f32[16,32]{1,0:T(8,128)S(1)} %get-tuple-element.15.scale_gate, ...), custom_call_target="tpu_custom_call" | custom-call | tf_op jit(solution)/shard_map/pallas_call | solution.py:360

commit v5 on v4

--- a/solution.py
+++ b/solution.py
@@ -62,6 +62,19 @@
     me, bank = lax.axis_index("zero"), lax.axis_index("bank")
     z, y = me // 4, lax.rem(me, 4)
 
+    barrier = pltpu.get_barrier_semaphore()
+
+    for k in range(PEERS - 1):
+        pl.semaphore_signal(
+            barrier, inc=1, device_id={"zero": far_first(k, me)}, device_id_type=MESH
+        )
+
+    for hop in range(1, BANKS):
+        pl.semaphore_signal(
+            barrier, inc=1, device_id={"bank": lax.rem(bank + hop, BANKS)}, device_id_type=MESH
+        )
+
+
     loads = []
     for n, (which, first) in enumerate(BLOCKS):
         copy = pltpu.make_async_copy(
@@ -74,18 +87,6 @@
         copy = pltpu.make_async_copy(source, target, load_sem.at[PAIRS + n])
         copy.start()
         small.append(copy)
-
-    barrier = pltpu.get_barrier_semaphore()
-
-    for k in range(PEERS - 1):
-        pl.semaphore_signal(
-            barrier, inc=1, device_id={"zero": far_first(k, me)}, device_id_type=MESH
-        )
-
-    for hop in range(1, BANKS):
-        pl.semaphore_signal(
-            barrier, inc=1, device_id={"bank": lax.rem(bank + hop, BANKS)}, device_id_type=MESH
-        )
 
     lane = lax.broadcasted_iota(jnp.int32, (8, 128), 1) // 32
 

time: 108 us -> 108 us (level)
  no operation moved by 1% of the time
where the time goes in v5:
time: 108 us; the launch traced here: 107 us
  Pallas kernels  106 us (98%)
    pallas_call x1, Pallas kernels, local(): pl.pallas_call(spread_kernel, out_shape=(jax.ShapeDtypeStruct((MATS, COLS...  104 us
    pallas_call x1, Pallas kernels, local(): pl.pallas_call(store_kernel, out_shape=(served, served, scale, scale, rou...  2.23 us

profile of v5, /device:TPU:10, one launch (start us, length us, event | category | flops | bytes accessed | tf_op | source)
XLA Modules:
  0.0 106.9 jit_solution(17726540409897294770)
XLA Ops:
  0.6 104.0 %shard_map.83 = (bf16[32,32,2048]{2,1,0:T(8,128)(2,1)S(1)}, f32[16,32]{1,0:T(8,128)S(1)}, f32[16,32]{1,0:T(8,128)S(1)}, bf16[4,16,2048]{2,1,0:T(8,128)(2,1)S(1)}) custom-call(f32[16,64,1024]{2,1,0:T(8,128)} %gate.1, f32[16,64,1024]{2,1,0:T(8,128)} %up.1, f32[16,64]{1,0:T(8,128)} %bitcast.7, f32[1,64]{1,0:T(1,128)} %bitcast.8), custom_call_target="tpu_custom_call" | custom-call | tf_op jit(solution)/shard_map/pallas_call | solution.py:323
  104.6 2.2 %shard_map.84 = (bf16[16,32,2048]{2,1,0:T(8,128)(2,1)}, bf16[16,32,2048]{2,1,0:T(8,128)(2,1)}, f32[16,32]{1,0:T(8,128)}, f32[16,32]{1,0:T(8,128)}, bf16[4,16,2048]{2,1,0:T(8,128)(2,1)}) custom-call(bf16[32,32,2048]{2,1,0:T(8,128)(2,1)S(1)} %get-tuple-element.14.placed, f32[16,32]{1,0:T(8,128)S(1)} %get-tuple-element.15.scale_gate, ...), custom_call_target="tpu_custom_call" | custom-call | tf_op jit(solution)/shard_map/pallas_call | solution.py:361
